TPU v7x, 32 devices: a whole 2x2x4 slice. The times are simulated.
32 devices in a mesh: grp: 2 (over x), tile: 16 (over z, y, core).
Axes of the slice: x: 2, y: 2, z: 4, core: 2. Of those that a mesh axis runs over, the one named last changes fastest.
Arguments:
- habitat: int32 [32, 4, 512], P(('grp', 'tile')), parts along dimension 0, may hold values from 0 to 15
- table: float32 [16], replicated, may hold values from 0.25 to 2
- source_cell: int32 [512], P('grp'), parts along dimension 0, may hold values from 0 to 32767
- ground_cell: int32 [512], P('grp'), parts along dimension 0, may hold values from 0 to 32767
- start_potential: float32 [32, 4, 512, 256], P(('grp', 'tile')), parts along dimension 0, may hold values from -30 to 30
Outputs:
- potentials: float32 [32, 4, 512, 256], P(('grp', 'tile')), parts along dimension 0
- residual: float32 [32, 4, 512, 256], P(('grp', 'tile')), parts along dimension 0
- resistance: float32 [512], P('grp'), parts along dimension 0
There are 2 independent parts, one for each index of `grp`. A program takes and returns all parts, laid end to end along the dimension named above; an argument that names none is the same for every part. Nothing has to cross between parts.
Inputs may be any that keep to these rules, and one draw needn't show every extreme that they name: `source_cell`: an index row * 1024 + column of the raster. `ground_cell`: an index row * 1024 + column of the raster.
All inputs are finite; a program needn't handle non-finite values.
Results may differ from a plain program's by a relative error of at most 0.00018.
Values sent between devices are 32-bit elements; how exact they have to be, the bound alone decides.
A program may use at most 128 MiB of HBM per device.

v0:
```python
import jax
import jax.numpy as jnp
from jax import lax
from jax.sharding import PartitionSpec as P

ITERS = 2


def shifted(block, axis, distance):
    devices = range(lax.axis_size(axis))
    route = [(i - distance, i) for i in devices if i - distance in devices]
    return lax.ppermute(block, axis, route)


def partner(value, axis, bit):
    mask = 2**bit
    pairs = [(source, source ^ mask) for source in range(lax.axis_size(axis))]
    return lax.ppermute(value, axis, pairs)


def column_sums(first, second):
    return jnp.sum(first * second, axis=(0, 1))


def shards(habitat, table, source_cell, ground_cell, start_potential):
    rows_here, cols_here = (habitat.shape[1], habitat.shape[2])
    block_id = lax.axis_index("tile")
    tile_count = lax.axis_size("tile")
    block_row = block_id // 2
    block_col = block_id % 2
    classes = habitat[0]
    levels = jnp.arange(table.shape[0], dtype=jnp.int32)
    conduct = jnp.sum(
        jnp.where(classes[:, :, None] == levels[None, None, :], table[None, None, :], 0.0), axis=2
    )
    inner_cond = jnp.where(block_col == 0, conduct[:, -1], conduct[:, 0])
    above_cond = shifted(conduct[-1], "tile", 2)
    below_cond = shifted(conduct[0], "tile", -2)
    side_cond = partner(inner_cond, "tile", 0)
    has_above = block_row > 0
    has_below = block_row < tile_count // 2 - 1
    row_index = jnp.arange(rows_here)[:, None]
    col_index = jnp.arange(cols_here)[None, :]
    upper_cond = jnp.concatenate([above_cond[None], conduct[:-1]], 0)
    lower_cond = jnp.concatenate([conduct[1:], below_cond[None]], 0)
    left_cond = jnp.concatenate([side_cond[:, None], conduct[:, :-1]], 1)
    right_cond = jnp.concatenate([conduct[:, 1:], side_cond[:, None]], 1)
    north_w = jnp.where((row_index > 0) | has_above, 0.5 * (conduct + upper_cond), 0.0)
    south_w = jnp.where((row_index < rows_here - 1) | has_below, 0.5 * (conduct + lower_cond), 0.0)
    west_w = jnp.where((col_index > 0) | (block_col == 1), 0.5 * (conduct + left_cond), 0.0)
    east_w = jnp.where(
        (col_index < cols_here - 1) | (block_col == 0), 0.5 * (conduct + right_cond), 0.0
    )
    global_rows = block_row * rows_here + jnp.arange(rows_here, dtype=jnp.int32)
    global_cols = block_col * cols_here + jnp.arange(cols_here, dtype=jnp.int32)
    cell_ids = global_rows[:, None] * (2 * cols_here) + global_cols[None, :]
    source_field = (cell_ids[:, :, None] == source_cell[None, None, :]).astype(jnp.float32)
    ground_field = (cell_ids[:, :, None] == ground_cell[None, None, :]).astype(jnp.float32)
    diagonal = (north_w + south_w + west_w + east_w)[:, :, None] + ground_field

    def operate(field):
        above = shifted(field[-1], "tile", 2)
        below = shifted(field[0], "tile", -2)
        inner_col = jnp.where(block_col == 0, field[:, -1], field[:, 0])
        side = partner(inner_col, "tile", 0)
        upper = jnp.concatenate([above[None], field[:-1]], 0)
        lower = jnp.concatenate([field[1:], below[None]], 0)
        leftward = jnp.concatenate([side[:, None], field[:, :-1]], 1)
        rightward = jnp.concatenate([field[:, 1:], side[:, None]], 1)
        applied = diagonal * field - north_w[:, :, None] * upper
        applied = applied - south_w[:, :, None] * lower
        applied = applied - west_w[:, :, None] * leftward
        return applied - east_w[:, :, None] * rightward

    potentials = start_potential[0]
    residual = source_field - operate(potentials)

    def paired(field, applied):
        return lax.psum((column_sums(field, field), column_sums(field, applied)), "tile")

    applied = operate(residual)
    norm_now, curve = paired(residual, applied)
    step_size = norm_now / curve
    direction, along = (residual, applied)
    for iteration in range(ITERS):
        potentials = potentials + step_size * direction
        residual = residual - step_size * along
        if iteration + 1 < ITERS:
            applied = operate(residual)
            norm_next, curve = paired(residual, applied)
            ratio = norm_next / norm_now
            step_size = norm_next / (curve - ratio * norm_next / step_size)
            direction = residual + ratio * direction
            along = applied + ratio * along
            norm_now = norm_next
    at_source, at_ground = lax.psum(
        (column_sums(potentials, source_field), column_sums(potentials, ground_field)), "tile"
    )
    return (potentials[None], residual[None], at_source - at_ground)


def solution(mesh):
    placed = (
        P(("grp", "tile"), None, None),
        P(),
        P("grp"),
        P("grp"),
        P(("grp", "tile"), None, None, None),
    )
    return jax.shard_map(
        shards,
        mesh=mesh,
        in_specs=placed,
        out_specs=(
            P(("grp", "tile"), None, None, None),
            P(("grp", "tile"), None, None, None),
            P("grp"),
        ),
        check_vma=False,
    )
```

profile of v0, /device:TPU:0, one launch (start us, length us, event | category | flops | bytes accessed | tf_op | source)
XLA Modules:
  0.0 214.9 jit_solution(9939268057922357837)
XLA Ops:
  0.7 1.0 select_reduce_fusion
  2.4 4.4 %collective-permute-start = (f32[512]{0:T(512)S(1)}, f32[512]{0:T(512)S(1)}, u32[]{:S(2)}, u32[]{:S(2)}) collective-permute-start(f32[512]{0:T(512)S(1)} %bitcast.91), channel_id=1, source_target_pairs={{0,2},{1,3},{2,4},{3,5},{4,6},{5,7},{6,8},{7,9},{8,10},{9,11},{10,... | collective-permute-start | bytes 6152 | tf_op jit(solution)/shard_map/ppermute | solution.py:12
  6.8 1.3 collective-permute-start.1
  8.1 2.3 %slice_bitcast_fusion.4 = (f32[512,256]{1,0:T(8,128)}, f32[512,256]{1,0:T(8,128)}) fusion(f32[1,4,512,256]{3,2,1,0:T(8,128)} %param.9), kind=kLoop, calls=%fused_computation.77 | loop fusion | bytes 2097152 | tf_op jit(solution)/shard_map/squeeze | solution.py:63
  10.4 1.3 collective-permute-start.4
  11.7 5.2 %collective-permute-start.3 = (f32[512,256]{1,0:T(8,128)}, f32[512,256]{1,0:T(8,128)S(1)}, u32[]{:S(2)}, u32[]{:S(2)}) collective-permute-start(f32[512,256]{1,0:T(8,128)} %get-tuple-element.64), channel_id=1, source_target_pairs={{0,2},{1,3},{2,4},{3,5},{4,6},{5,7},{6,8},{7,9},{8,10},{9,11},{10,... | collective-permute-start | bytes 1572872 | tf_op jit(solution)/shard_map/ppermute | solution.py:12
  17.0 2.9 %fusion.58 = (f32[1,3,512,256]{3,2,1,0:T(8,128)}, f32[3,512,256]{2,1,0:T(8,128)}, f32[3,512,256]{2,1,0:T(8,128)}, f32[1,3,512,256]{3,2,1,0:T(8,128)}) fusion(f32[1,4,512,256]{3,2,1,0:T(8,128)S(1)} %copy-done), kind=kLoop, calls=%fused_computation.124 | loop fusion | bytes 9437184 | tf_op jit(solution)/shard_map/slice | solution.py:66
  19.9 3.7 %slice_bitcast_fusion.17 = (f32[1,4,511,256]{3,2,1,0:T(8,128)}, f32[1,4,511,256]{3,2,1,0:T(8,128)}, f32[4,511,256]{2,1,0:T(8,128)}, f32[4,511,256]{2,1,0:T(8,128)}) fusion(f32[4,512,256]{2,1,0:T(8,128)S(1)} %bitcast.69), kind=kLoop, calls=%fused_computation.123 | loop fusion | bytes 12558336 | tf_op jit(solution)/shard_map/concatenate | solution.py:68
  24.0 1.0 collective-permute-done.5
  25.0 2.1 collective-permute-done.4
  27.1 11.5 %collective-permute-done.3 = f32[512,256]{1,0:T(8,128)S(1)} collective-permute-done((f32[512,256]{1,0:T(8,128)}, f32[512,256]{1,0:T(8,128)S(1)}, u32[]{:S(2)}, u32[]{:S(2)}) %collective-permute-start.3) | collective-permute-done | bytes 524320 | tf_op jit(solution)/shard_map/ppermute | solution.py:12
  38.6 4.7 %fusion = f32[4,512,256]{2,1,0:T(8,128)S(1)} fusion(f32[3,512,256]{2,1,0:T(8,128)} %get-tuple-element.30, f32[1,512,256]{2,1,0:T(8,128)S(1)} %bitcast.72, f32[1,512,256]{2,1,0:T(8,128)S(1)} %bitcast.70, f32[3,512,256]{2,1,0:T(8,128)} %get-tuple-element.31, f32[4,511,256]{2,1,0:T(8,128)} %get-tuple-element.35, f32[4,1,256]{2,1,0:T(1,128)S(1)} %copy.106, ...), kind=kLoop, calls=%fused_computation.4 | loop fusion | flops 9961472 | bytes 12630016 | tf_op jit(solution)/shard_map/sub | solution.py:76
  43.4 2.6 %slice_bitcast_fusion.15 = (f32[1,4,511,256]{3,2,1,0:T(8,128)}, f32[4,511,256]{2,1,0:T(8,128)S(1)}, f32[4,511,256]{2,1,0:T(8,128)S(1)}, f32[1,4,511,256]{3,2,1,0:T(8,128)}) fusion(f32[4,512,256]{2,1,0:T(8,128)S(1)} %fusion), kind=kLoop, calls=%fused_computation.121 | loop fusion | bytes 12558336 | tf_op jit(solution)/shard_map/concatenate | solution.py:68
  46.0 4.3 %collective-permute-start.6 = (f32[512,256]{1,0:T(8,128)S(1)}, f32[512,256]{1,0:T(8,128)S(1)}, u32[]{:S(2)}, u32[]{:S(2)}) collective-permute-start(f32[512,256]{1,0:T(8,128)S(1)} %get-tuple-element.57), channel_id=1, source_target_pairs={{0,2},{1,3},{2,4},{3,5},{4,6},{5,7},{6,8},{7,9},{8,10},{9,11},{10,... | collective-permute-start | bytes 1572872 | tf_op jit(solution)/shard_map/ppermute | solution.py:12
  50.3 1.3 collective-permute-start.7
  51.7 2.3 %slice_bitcast_fusion.9 = (f32[1,3,512,256]{3,2,1,0:T(8,128)}, f32[1,3,512,256]{3,2,1,0:T(8,128)}, f32[3,512,256]{2,1,0:T(8,128)S(1)}, f32[3,512,256]{2,1,0:T(8,128)S(1)}) fusion(f32[4,512,256]{2,1,0:T(8,128)S(1)} %fusion), kind=kLoop, calls=%fused_computation.115 | loop fusion | bytes 9437184 | tf_op jit(solution)/shard_map/concatenate | solution.py:66
  54.0 18.9 %collective-permute-done.6 = f32[512,256]{1,0:T(8,128)S(1)} collective-permute-done((f32[512,256]{1,0:T(8,128)S(1)}, f32[512,256]{1,0:T(8,128)S(1)}, u32[]{:S(2)}, u32[]{:S(2)}) %collective-permute-start.6) | collective-permute-done | bytes 524320 | tf_op jit(solution)/shard_map/ppermute | solution.py:12
  72.9 3.5 %multiply_reduce_fusion.1 = (f32[256]{0:T(256)S(1)}, f32[256]{0:T(256)S(1)}, f32[4,512,256]{2,1,0:T(8,128)}) fusion(f32[4,512,256]{2,1,0:T(8,128)S(1)} %fusion, f32[4,1,256]{2,1,0:T(1,128)S(1)} %broadcast_in_dim.123, f32[4,511,256]{2,1,0:T(8,128)S(1)} %get-tuple-element.42, f32[4,512]{1,0:T(4,128)S(1)} %get-tuple-element.28, ...), kind=kLoop, calls=%fused_computation.71 | loop fusion | flops 10485248 | bytes 12631040 | tf_op jit(solution)/shard_map/reduce_sum | solution.py:22
  76.3 32.6 %all-reduce.2 = (f32[256]{0:T(256)S(1)}, f32[256]{0:T(256)S(1)}) all-reduce(f32[256]{0:T(256)S(1)} %get-tuple-element.11, f32[256]{0:T(256)S(1)} %get-tuple-element.10), channel_id=1, replica_groups=mesh['grp'=2,'tile'=16] {'tile'}, use_global_device_ids=true, to_apply=%region_2.3 | all-reduce | flops 512 | bytes 4096 | tf_op jit(solution)/shard_map/psum | solution.py:79
  108.9 2.5 %multiply_subtract_fusion.1 = f32[4,512,256]{2,1,0:T(8,128)S(1)} fusion(f32[4,512,256]{2,1,0:T(8,128)} %copy-done.1, f32[4,512,256]{2,1,0:T(8,128)} %get-tuple-element.23, f32[256]{0:T(256)S(1)} %div.23), kind=kLoop, calls=%fused_computation.69 | loop fusion | flops 1048576 | bytes 6292480 | tf_op jit(solution)/shard_map/sub | solution.py:87
  111.5 2.5 %fusion.59 = (f32[4,511,256]{2,1,0:T(8,128)S(1)}, f32[1,4,511,256]{3,2,1,0:T(8,128)}, f32[4,511,256]{2,1,0:T(8,128)S(1)}, f32[1,4,511,256]{3,2,1,0:T(8,128)}) fusion(f32[4,512,256]{2,1,0:T(8,128)S(1)} %multiply_subtract_fusion.1), kind=kLoop, calls=%fused_computation.125 | loop fusion | bytes 12558336 | tf_op jit(solution)/shard_map/slice | solution.py:69
  114.1 1.3 collective-permute-start.10
  115.3 4.6 %collective-permute-start.9 = (f32[512,256]{1,0:T(8,128)S(1)}, f32[512,256]{1,0:T(8,128)S(1)}, u32[]{:S(2)}, u32[]{:S(2)}) collective-permute-start(f32[512,256]{1,0:T(8,128)S(1)} %get-tuple-element.56), channel_id=1, source_target_pairs={{0,2},{1,3},{2,4},{3,5},{4,6},{5,7},{6,8},{7,9},{8,10},{9,11},{10,... | collective-permute-start | bytes 1572872 | tf_op jit(solution)/shard_map/ppermute | solution.py:12
  120.0 2.3 %fusion.60 = (f32[3,512,256]{2,1,0:T(8,128)S(1)}, f32[1,3,512,256]{3,2,1,0:T(8,128)}, f32[1,3,512,256]{3,2,1,0:T(8,128)}, f32[3,512,256]{2,1,0:T(8,128)S(1)}) fusion(f32[4,512,256]{2,1,0:T(8,128)S(1)} %multiply_subtract_fusion.1), kind=kLoop, calls=%fused_computation.126 | loop fusion | bytes 9437184 | tf_op jit(solution)/shard_map/slice | solution.py:67
  122.3 4.2 %collective-permute-done.10 = f32[512,256]{1,0:T(8,128)S(1)} collective-permute-done((f32[512,256]{1,0:T(8,128)S(1)}, f32[512,256]{1,0:T(8,128)S(1)}, u32[]{:S(2)}, u32[]{:S(2)}) %collective-permute-start.10) | collective-permute-done | bytes 524320 | tf_op jit(solution)/shard_map/ppermute | solution.py:12
  126.6 6.7 %collective-permute-done.9 = f32[512,256]{1,0:T(8,128)S(1)} collective-permute-done((f32[512,256]{1,0:T(8,128)S(1)}, f32[512,256]{1,0:T(8,128)S(1)}, u32[]{:S(2)}, u32[]{:S(2)}) %collective-permute-start.9) | collective-permute-done | bytes 524320 | tf_op jit(solution)/shard_map/ppermute | solution.py:12
  133.3 2.4 %fusion.19 = (f32[256]{0:T(256)S(1)}, f32[256]{0:T(256)S(1)}) fusion(f32[4,512,256]{2,1,0:T(8,128)S(1)} %multiply_subtract_fusion.1, f32[3,512,256]{2,1,0:T(8,128)S(1)} %get-tuple-element.52, f32[1,512,256]{2,1,0:T(8,128)S(1)} %bitcast.80, f32[1,512,256]{2,1,0:T(8,128)S(1)} %bitcast.78, f32[3,512,256]{2,1,0:T(8,128)S(1)} %get-tuple-element.49, ...), kind=kLoop, calls=%fused_computation.23 | loop fusion | flops 10485248 | bytes 10533888 | tf_op jit(solution)/shard_map/reduce_sum | solution.py:22
  135.7 31.9 %all-reduce.1 = (f32[256]{0:T(256)S(1)}, f32[256]{0:T(256)S(1)}) all-reduce(f32[256]{0:T(256)S(1)} %get-tuple-element.9, f32[256]{0:T(256)S(1)} %get-tuple-element.8), channel_id=1, replica_groups=mesh['grp'=2,'tile'=16] {'tile'}, use_global_device_ids=true, to_apply=%region_6.7 | all-reduce | flops 512 | bytes 4096 | tf_op jit(solution)/shard_map/psum | solution.py:79
  167.6 2.6 %fusion.20 = (f32[256]{0:T(256)S(1)}, f32[256]{0:T(256)S(1)}) fusion(s32[256]{0:T(256)S(1)} %copy-done.7, s32[4,512]{1,0:T(4,128)S(1)} %broadcast_add_fusion, s32[256]{0:T(256)S(1)} %copy-done.8, f32[4,512,256]{2,1,0:T(8,128)} %copy-done.2, f32[4,512,256]{2,1,0:T(8,128)} %copy-done.1, f32[256]{0:T(256)S(1)} %get-tuple-element.22, ...), kind=kLoop, calls=%fused_computation.24 | loop fusion | flops 6290944 | bytes 6306816 | tf_op jit(solution)/shard_map/reduce_sum | solution.py:22
  170.2 29.5 %all-reduce = (f32[256]{0:T(256)S(1)}, f32[256]{0:T(256)S(1)}) all-reduce(f32[256]{0:T(256)S(1)} %get-tuple-element.7, f32[256]{0:T(256)S(1)} %get-tuple-element.6), channel_id=1, replica_groups=mesh['grp'=2,'tile'=16] {'tile'}, use_global_device_ids=true, to_apply=%region_10.11 | all-reduce | flops 512 | bytes 4096 | tf_op jit(solution)/shard_map/psum | solution.py:96
  200.3 12.8 %fusion.36 = (f32[1,4,512,256]{3,2,1,0:T(8,128)}, f32[1,4,512,256]{3,2,1,0:T(8,128)S(1)}, f32[1,4,512,256]{3,2,1,0:T(8,128)S(1)}) fusion(f32[1,3,512,256]{3,2,1,0:T(8,128)} %get-tuple-element.50, f32[1,1,512,256]{3,2,1,0:T(8,128)} %bitcast.81, f32[1,1,512,256]{3,2,1,0:T(8,128)} %bitcast.79, f32[1,3,512,256]{3,2,1,0:T(8,128)} %get-tuple-element.51, ...), kind=kLoop, calls=%fused_computation.61 | loop fusion | flops 26738688 | bytes 33596416 | tf_op jit(solution)/shard_map/sub | solution.py:87
  213.1 1.9 multiply_add_fusion.1
  (57 shorter events, 2.2 us)
Async XLA Ops:
  0.6 16.3 %copy-start = (f32[1,4,512,256]{3,2,1,0:T(8,128)S(1)}, f32[1,4,512,256]{3,2,1,0:T(8,128)}, u32[]{:S(2)}) copy-start(f32[1,4,512,256]{3,2,1,0:T(8,128)} %param.9) | copy-start | bytes 6291460
  1.8 21.9 %collective-permute-start.2 = (f32[4]{0:T(128)S(1)}, f32[4]{0:T(128)S(1)}, u32[]{:S(2)}, u32[]{:S(2)}) collective-permute-start(f32[4]{0:T(128)S(1)} %fusion.48), channel_id=1, source_target_pairs={{0,1},{1,0},{2,3},{3,2},{4,5},{5,4},{6,7},{7,6},{8,9},{9,8},{10,11... | collective-permute-start | bytes 56 | tf_op jit(solution)/shard_map/ppermute | solution.py:18
  2.4 21.6 %collective-permute-start = (f32[512]{0:T(512)S(1)}, f32[512]{0:T(512)S(1)}, u32[]{:S(2)}, u32[]{:S(2)}) collective-permute-start(f32[512]{0:T(512)S(1)} %bitcast.91), channel_id=1, source_target_pairs={{0,2},{1,3},{2,4},{3,5},{4,6},{5,7},{6,8},{7,9},{8,10},{9,11},{10,... | collective-permute-start | bytes 6152 | tf_op jit(solution)/shard_map/ppermute | solution.py:12
  6.8 17.1 %collective-permute-start.1 = (f32[512]{0:T(512)S(1)}, f32[512]{0:T(512)S(1)}, u32[]{:S(2)}, u32[]{:S(2)}) collective-permute-start(f32[512]{0:T(512)S(1)} %bitcast.90), channel_id=1, source_target_pairs={{2,0},{3,1},{4,2},{5,3},{6,4},{7,5},{8,6},{9,7},{10,8},{11,9},{12,... | collective-permute-start | bytes 6152 | tf_op jit(solution)/shard_map/ppermute | solution.py:12
  10.4 16.7 %collective-permute-start.4 = (f32[512,256]{1,0:T(8,128)}, f32[512,256]{1,0:T(8,128)S(1)}, u32[]{:S(2)}, u32[]{:S(2)}) collective-permute-start(f32[512,256]{1,0:T(8,128)} %get-tuple-element.63), channel_id=1, source_target_pairs={{2,0},{3,1},{4,2},{5,3},{6,4},{7,5},{8,6},{9,7},{10,8},{11,9},{12,... | collective-permute-start | bytes 1572872 | tf_op jit(solution)/shard_map/ppermute | solution.py:12
  11.7 26.9 %collective-permute-start.3 = (f32[512,256]{1,0:T(8,128)}, f32[512,256]{1,0:T(8,128)S(1)}, u32[]{:S(2)}, u32[]{:S(2)}) collective-permute-start(f32[512,256]{1,0:T(8,128)} %get-tuple-element.64), channel_id=1, source_target_pairs={{0,2},{1,3},{2,4},{3,5},{4,6},{5,7},{6,8},{7,9},{8,10},{9,11},{10,... | collective-permute-start | bytes 1572872 | tf_op jit(solution)/shard_map/ppermute | solution.py:12
  19.9 18.7 %copy-start.7 = (s32[256]{0:T(256)S(1)}, s32[256]{0:T(256)}, u32[]{:S(2)}) copy-start(s32[256]{0:T(256)} %param.8) | copy-start | bytes 3076
  19.9 18.7 %copy-start.8 = (s32[256]{0:T(256)S(1)}, s32[256]{0:T(256)}, u32[]{:S(2)}) copy-start(s32[256]{0:T(256)} %param.7) | copy-start | bytes 3076
  23.8 1.2 collective-permute-start.5
  43.3 29.6 %copy-start.1 = (f32[4,512,256]{2,1,0:T(8,128)}, f32[4,512,256]{2,1,0:T(8,128)S(1)}, u32[]{:S(2)}) copy-start(f32[4,512,256]{2,1,0:T(8,128)S(1)} %fusion) | copy-start | bytes 6291460
  46.0 26.9 %collective-permute-start.6 = (f32[512,256]{1,0:T(8,128)S(1)}, f32[512,256]{1,0:T(8,128)S(1)}, u32[]{:S(2)}, u32[]{:S(2)}) collective-permute-start(f32[512,256]{1,0:T(8,128)S(1)} %get-tuple-element.57), channel_id=1, source_target_pairs={{0,2},{1,3},{2,4},{3,5},{4,6},{5,7},{6,8},{7,9},{8,10},{9,11},{10,... | collective-permute-start | bytes 1572872 | tf_op jit(solution)/shard_map/ppermute | solution.py:12
  50.3 22.6 %collective-permute-start.7 = (f32[512,256]{1,0:T(8,128)S(1)}, f32[512,256]{1,0:T(8,128)S(1)}, u32[]{:S(2)}, u32[]{:S(2)}) collective-permute-start(f32[512,256]{1,0:T(8,128)S(1)} %get-tuple-element.58), channel_id=1, source_target_pairs={{2,0},{3,1},{4,2},{5,3},{6,4},{7,5},{8,6},{9,7},{10,8},{11,9},{12,... | collective-permute-start | bytes 1572872 | tf_op jit(solution)/shard_map/ppermute | solution.py:12
  51.6 2.3 %collective-permute-start.8 = (f32[4,256]{1,0:T(4,128)S(1)}, f32[4,256]{1,0:T(4,128)S(1)}, u32[]{:S(2)}, u32[]{:S(2)}) collective-permute-start(f32[4,256]{1,0:T(4,128)S(1)} %fusion.46), channel_id=1, source_target_pairs={{0,1},{1,0},{2,3},{3,2},{4,5},{5,4},{6,7},{7,6},{8,9},{9,8},{10,11... | collective-permute-start | bytes 12296 | tf_op jit(solution)/shard_map/ppermute | solution.py:18
  72.9 3.5 %copy-start.3 = (f32[512,256]{1,0:T(8,128)}, f32[512,256]{1,0:T(8,128)S(1)}, u32[]{:S(2)}) copy-start(f32[512,256]{1,0:T(8,128)S(1)} %collective-permute-done.6) | copy-start | bytes 1572868
  72.9 3.5 %copy-start.4 = (f32[512,256]{1,0:T(8,128)}, f32[512,256]{1,0:T(8,128)S(1)}, u32[]{:S(2)}) copy-start(f32[512,256]{1,0:T(8,128)S(1)} %collective-permute-done.7) | copy-start | bytes 1572868
  111.4 21.9 %copy-start.2 = (f32[4,512,256]{2,1,0:T(8,128)}, f32[4,512,256]{2,1,0:T(8,128)S(1)}, u32[]{:S(2)}) copy-start(f32[4,512,256]{2,1,0:T(8,128)S(1)} %multiply_subtract_fusion.1) | copy-start | bytes 6291460
  114.1 12.5 %collective-permute-start.10 = (f32[512,256]{1,0:T(8,128)S(1)}, f32[512,256]{1,0:T(8,128)S(1)}, u32[]{:S(2)}, u32[]{:S(2)}) collective-permute-start(f32[512,256]{1,0:T(8,128)S(1)} %get-tuple-element.55), channel_id=1, source_target_pairs={{2,0},{3,1},{4,2},{5,3},{6,4},{7,5},{8,6},{9,7},{10,8},{11,9},{12,... | collective-permute-start | bytes 1572872 | tf_op jit(solution)/shard_map/ppermute | solution.py:12
  115.3 17.9 %collective-permute-start.9 = (f32[512,256]{1,0:T(8,128)S(1)}, f32[512,256]{1,0:T(8,128)S(1)}, u32[]{:S(2)}, u32[]{:S(2)}) collective-permute-start(f32[512,256]{1,0:T(8,128)S(1)} %get-tuple-element.56), channel_id=1, source_target_pairs={{0,2},{1,3},{2,4},{3,5},{4,6},{5,7},{6,8},{7,9},{8,10},{9,11},{10,... | collective-permute-start | bytes 1572872 | tf_op jit(solution)/shard_map/ppermute | solution.py:12
  119.9 2.4 %collective-permute-start.11 = (f32[4,256]{1,0:T(4,128)S(1)}, f32[4,256]{1,0:T(4,128)S(1)}, u32[]{:S(2)}, u32[]{:S(2)}) collective-permute-start(f32[4,256]{1,0:T(4,128)S(1)} %fusion.45), channel_id=1, source_target_pairs={{0,1},{1,0},{2,3},{3,2},{4,5},{5,4},{6,7},{7,6},{8,9},{9,8},{10,11... | collective-permute-start | bytes 12296 | tf_op jit(solution)/shard_map/ppermute | solution.py:18
  126.5 9.1 %copy-start.5 = (f32[512,256]{1,0:T(8,128)}, f32[512,256]{1,0:T(8,128)S(1)}, u32[]{:S(2)}) copy-start(f32[512,256]{1,0:T(8,128)S(1)} %collective-permute-done.10) | copy-start | bytes 1572868
  133.3 2.4 %copy-start.6 = (f32[512,256]{1,0:T(8,128)}, f32[512,256]{1,0:T(8,128)S(1)}, u32[]{:S(2)}) copy-start(f32[512,256]{1,0:T(8,128)S(1)} %collective-permute-done.9) | copy-start | bytes 1572868
where the time goes:
time: 215 us
  blocking collectives  94 us (44%)
  waiting for transfers between devices  44.4 us (21%)
  other arithmetic  32.2 us (15%)
  starting transfers between devices  24.4 us (11%)
  local copies, waits for them, and re-layouts  19 us (9%)
    psum x2, blocking collectives, paired(): lax.psum((column_sums(field, field), column_sums(field, applied)), 'tile')  64.5 us
    ppermute x8, waiting for transfers between devices, shifted(): return lax.ppermute(block, axis, route)  43.4 us
    psum x1, blocking collectives, shards(): lax.psum((column_sums(potentials, source_field), column_sums(potentials,...  29.5 us
    ppermute x8, starting transfers between devices, shifted(): return lax.ppermute(block, axis, route)  23.7 us
    sub x2, other arithmetic, shards(): residual = residual - step_size * along  15.3 us
    reduce_sum x3, other arithmetic, column_sums(): return jnp.sum(first * second, axis=(0, 1))  8.45 us
    concatenate x5, local copies, waits for them, and re-layouts, operate(): leftward = jnp.concatenate([side[:, None], field[:, :-1]], 1)  6.32 us
    sub x1, other arithmetic, shards(): residual = source_field - operate(potentials)  4.66 us
  transfers between devices with their start and end apart: 12, of which 6 were waited for; matrix products, arithmetic and copies ran while one was open for 6% of the time, Pallas kernels for 0%

commit v1 on v0

v1 whole, which is shorter than its diff:
```python
import functools

import jax
import jax.numpy as jnp
from jax import lax
from jax.experimental import pallas as pl
from jax.experimental.pallas import tpu as pltpu
from jax.sharding import PartitionSpec as P

LANES = 128
TILE = 8
PAD = 2 * TILE
MESH = pl.DeviceIdType.MESH


def kernel(n, rows, cols, table_ref, habitat_ref, source_ref, ground_ref, start_ref,
           pot_ref, res_ref, drop_ref,
           X, R, W, U, V, H, D, C, T, TV, TH, S, O1, O2,
           load_sem, cond_send, cond_recv, side_send, side_recv,
           row_send, row_recv, relay_send, relay_recv, sum_send, sum_recv, out_sem):
    halves = X.shape[0]
    width = cols + 2 * PAD
    me = lax.axis_index("tile")
    chips = n // 2
    chip = me // 2
    core = me % 2
    odd = chip % 2
    side = me + 1 - 2 * core
    partner = me + 2 - 4 * odd
    own = pl.ds(PAD, cols)

    def load(h):
        return pltpu.make_async_copy(
            start_ref.at[0, :, :, pl.ds(h * LANES, LANES)], X.at[h, pl.ds(rows, rows), own, :],
            load_sem.at[h])

    for h in range(halves):
        load(h).start()

    barrier = pltpu.get_barrier_semaphore()

    def greet(d, _):
        pl.semaphore_signal(barrier, inc=1, device_id={"tile": (me + d) % n}, device_id_type=MESH)
        return 0

    cells = habitat_ref[0]
    cond = jnp.zeros(cells.shape, jnp.float32)
    for level in range(table_ref.shape[0]):
        cond = jnp.where(cells == level, table_ref[level], cond)
    for slot in range(5):
        C[slot] = jnp.zeros(C.shape[1:], jnp.float32)
    C[5, 0:rows, :] = cond
    C[5, rows:2 * rows, :] = cond

    def zero(ref, lead, c):
        count = ref.shape[1]
        ref[lead[0], :, c:c + TILE, :] = jnp.zeros((count, TILE, LANES), jnp.float32)

    for h in range(halves):
        for c in (0, width - TILE):
            zero(X, (h,), c)
            zero(R, (h,), c)
            zero(W, (h,), c)
        @pl.when(core == 0)
        def _():
            zero(X, (h,), TILE)
        @pl.when(core == 1)
        def _():
            zero(X, (h,), width - PAD)
        @pl.when(chip == 0)
        def _():
            X[h, 0:rows] = jnp.zeros((rows, width, LANES), jnp.float32)
        @pl.when(chip == chips - 1)
        def _():
            X[h, 2 * rows:3 * rows] = jnp.zeros((rows, width, LANES), jnp.float32)

    lax.fori_loop(1, n, greet, 0)
    pl.semaphore_wait(barrier, n - 1)

    def cond_copy(target, slot):
        return pltpu.make_async_remote_copy(
            src_ref=C.at[5], dst_ref=C.at[slot], send_sem=cond_send.at[slot],
            recv_sem=cond_recv.at[slot], device_id={"tile": target}, device_id_type=MESH)

    has_above = chip > 0
    has_below = chip < chips - 1

    def cond_each(act):
        act(cond_copy(side, 2))

        @pl.when(has_above)
        def _():
            act(cond_copy(me - 2, 1))
            act(cond_copy(side - 2, 4))

        @pl.when(has_below)
        def _():
            act(cond_copy(me + 2, 0))
            act(cond_copy(side + 2, 3))

    cond_each(lambda copy: copy.start())

    inner = pl.multiple_of(PAD + (1 - core) * (cols - TILE), TILE)

    def side_copy(h):
        dst = pl.multiple_of((1 - core) * TILE + core * (PAD + cols), TILE)
        return pltpu.make_async_remote_copy(
            src_ref=X.at[h, pl.ds(rows, rows), pl.ds(inner, TILE), :],
            dst_ref=X.at[h, pl.ds(rows, rows), pl.ds(dst, TILE), :],
            send_sem=side_send.at[h], recv_sem=side_recv.at[h],
            device_id={"tile": side}, device_id_type=MESH)

    span = pl.ds(pl.multiple_of(PAD - core * TILE, TILE), cols + TILE)

    def row_copy(h, i):
        r = (i + odd) % rows
        return pltpu.make_async_remote_copy(
            src_ref=X.at[h, rows + r, span, :], dst_ref=X.at[h, odd * 2 * rows + r, span, :],
            send_sem=row_send.at[h, i], recv_sem=row_recv.at[h, i],
            device_id={"tile": partner}, device_id_type=MESH)

    def row_wait(h, i):
        r = (i + 1 - odd) % rows
        place = X.at[h, (1 - odd) * 2 * rows + r, span, :]
        pltpu.make_async_remote_copy(
            src_ref=place, dst_ref=place, send_sem=row_send.at[h, i], recv_sem=row_recv.at[h, i],
            device_id={"tile": partner}, device_id_type=MESH).wait_recv()

    relay_to = me + 4 - 8 * odd
    can_relay = jnp.where(odd == 0, chip + 2 < chips, chip >= 2)
    gets_relay = jnp.where(odd == 0, chip >= 2, chip + 2 < chips)

    def relay_copy(h, i):
        src = (1 - odd) * (2 * rows + 1) + i
        dst = odd * 2 * rows + (1 - odd) + i
        return pltpu.make_async_remote_copy(
            src_ref=X.at[h, src, span, :], dst_ref=X.at[h, dst, span, :],
            send_sem=relay_send.at[h, i], recv_sem=relay_recv.at[h, i],
            device_id={"tile": relay_to}, device_id_type=MESH)

    def relay_wait(h):
        @pl.when(gets_relay)
        def _():
            for i in range(rows - 1):
                dst = odd * 2 * rows + (1 - odd) + i
                place = X.at[h, dst, span, :]
                pltpu.make_async_remote_copy(
                    src_ref=place, dst_ref=place, send_sem=relay_send.at[h, i],
                    recv_sem=relay_recv.at[h, i],
                    device_id={"tile": relay_to}, device_id_type=MESH).wait_recv()

    def take(h, i):
        row_wait(h, i)
        if i < rows - 1:
            @pl.when(can_relay)
            def _():
                relay_copy(h, i).start()

    for h in range(halves):
        load(h).wait()
        side_copy(h).start()
    for h in range(halves):
        side_copy(h).wait_recv()
        for i in range(rows):
            row_copy(h, i).start()

    cond_copy(side, 2).wait_recv()

    @pl.when(has_above)
    def _():
        cond_copy(me - 2, 0).wait_recv()
        cond_copy(side - 2, 3).wait_recv()

    @pl.when(has_below)
    def _():
        cond_copy(me + 2, 1).wait_recv()
        cond_copy(side + 2, 4).wait_recv()

    first = lax.broadcasted_iota(jnp.int32, (2 * rows, LANES), 0) < rows

    def turned(above, here, below, j):
        lanes = slice(j * LANES, (j + 1) * LANES)
        top = jnp.where(first, C[above, :, lanes], C[here, :, lanes])
        blank = jnp.zeros((LANES - 4 * rows, LANES), jnp.float32)
        return jnp.transpose(jnp.concatenate([top, C[below, :, lanes], blank], 0))

    for j in range(cols // LANES):
        T[PAD + j * LANES:PAD + (j + 1) * LANES, :] = turned(0, 5, 1, j)
    for c in (0, TILE, width - PAD, width - TILE):
        T[c:c + TILE, :] = jnp.zeros((TILE, LANES), jnp.float32)

    @pl.when(core == 0)
    def _():
        T[width - PAD:width - TILE, :] = turned(3, 2, 4, 0)[0:TILE]

    @pl.when(core == 1)
    def _():
        T[TILE:PAD, :] = turned(3, 2, 4, cols // LANES - 1)[LANES - TILE:]

    def global_col(c):
        return core * cols - PAD + c + lax.broadcasted_iota(jnp.int32, (TILE, LANES), 0)

    global_row = chip * rows - rows + lax.broadcasted_iota(jnp.int32, (TILE, LANES), 1)
    total_rows, total_cols = chips * rows, 2 * cols

    def edges(t, _):
        c = pl.multiple_of(t * TILE, TILE)
        here = T[pl.ds(c, TILE), :]
        east = T[pl.ds(c + 1, TILE), :]
        south = pltpu.roll(here, LANES - 1, 1)
        gc = global_col(c)
        in_row = (global_row >= 0) & (global_row < total_rows - 1)
        TV[pl.ds(c, TILE), :] = jnp.where(in_row, 0.5 * (here + south), 0.0)
        in_col = (gc >= 0) & (gc < total_cols - 1)
        TH[pl.ds(c, TILE), :] = jnp.where(in_col, 0.5 * (here + east), 0.0)
        return 0

    TH[0:TILE, :] = jnp.zeros((TILE, LANES), jnp.float32)
    H[:, 0:TILE, :] = jnp.zeros((H.shape[0], TILE, LANES), jnp.float32)
    lax.fori_loop(1, width // TILE - 1, edges, 0)

    def spread(t, _):
        c = pl.multiple_of(t * TILE, TILE)
        at = pl.ds(c, TILE)
        v = TV[at, :]
        east = TH[at, :]
        west = TH[pl.ds(c - 1, TILE), :]
        diag = v + pltpu.roll(v, 1, 1) + east + west
        shape = (TILE, LANES)
        for k in range(2 * rows + 1):
            V[k, at, :] = jnp.broadcast_to(v[:, k + 1:k + 2], shape)
        for k in range(2 * rows):
            H[k, at, :] = jnp.broadcast_to(east[:, k + 2:k + 3], shape)
            D[k, at, :] = jnp.broadcast_to(diag[:, k + 2:k + 3], shape)
        return 0

    lax.fori_loop(1, width // TILE - 1, spread, 0)

    def cell_ids(c, count, top):
        shape = (count, TILE, LANES)
        r = chip * rows + top + lax.broadcasted_iota(jnp.int32, shape, 0)
        col = core * cols - PAD + c + lax.broadcasted_iota(jnp.int32, shape, 1)
        return r * total_cols + col

    def applied(ref, h, skip, count, c, low, grounded):
        at = pl.ds(c, TILE)
        f = ref[h, skip:skip + count + 2, at, :]
        left = ref[h, skip + 1:skip + 1 + count, pl.ds(c - 1, TILE), :]
        right = ref[h, skip + 1:skip + 1 + count, pl.ds(c + 1, TILE), :]
        mid = f[1:count + 1]
        v = V[low:low + count + 1, at, :]
        out = D[low:low + count, at, :] * mid + jnp.where(grounded, mid, 0.0)
        out = out - v[:count] * f[:count] - v[1:] * f[2:]
        out = out - H[low:low + count, pl.ds(c - 1, TILE), :] * left
        return out - H[low:low + count, at, :] * right, mid

    def compute(h):
        src = source_ref[h:h + 1, :][None]
        gnd = ground_ref[h:h + 1, :][None]
        inner_rows = 2 * rows

        def pass_r(t, _):
            c = pl.multiple_of(t * TILE, TILE)
            ids = cell_ids(c, inner_rows, -2)
            a, _mid = applied(X, h, 1, inner_rows, c, 0, ids == gnd)
            R[h, :, pl.ds(c, TILE), :] = jnp.where(ids == src, 1.0, 0.0) - a
            return 0

        def pass_w(t, _):
            c = pl.multiple_of(t * TILE, TILE)
            count = inner_rows - 2
            ids = cell_ids(c, count, -1)
            a, _mid = applied(R, h, 0, count, c, 1, ids == gnd)
            W[h, :, pl.ds(c, TILE), :] = a
            return 0

        def pass_u(t, acc):
            c = pl.multiple_of(t * TILE, TILE)
            at = pl.ds(c, TILE)
            ids = cell_ids(c, rows, 0)
            is_g = ids == gnd
            u, w = applied(W, h, 0, rows, c, 2, is_g)
            U[h, :, pl.ds(c - PAD, TILE), :] = u
            r = R[h, 2:2 + rows, at, :]
            x = X[h, rows:2 * rows, at, :]
            sign = jnp.where(ids == src, 1.0, 0.0) - jnp.where(is_g, 1.0, 0.0)
            terms = (r * r, r * w, w * w, w * u, sign * x, sign * r, sign * w)
            return tuple(s + jnp.sum(term, axis=0) for s, term in zip(acc, terms))

        tiles = width // TILE
        lax.fori_loop(1, tiles - 1, pass_r, 0)
        lax.fori_loop(1, tiles - 1, pass_w, 0)
        acc = lax.fori_loop(2, tiles - 2, pass_u,
                            tuple(jnp.zeros((TILE, LANES), jnp.float32) for _ in range(7)))
        sums = [jnp.sum(s, axis=0, keepdims=True) for s in acc]
        S[h, me] = jnp.concatenate(sums + [jnp.zeros((1, LANES), jnp.float32)], 0)

    def sum_copy(h, d):
        return pltpu.make_async_remote_copy(
            src_ref=S.at[h, me], dst_ref=S.at[h, me], send_sem=sum_send.at[h, d],
            recv_sem=sum_recv.at[h, d],
            device_id={"tile": (me + d) % n}, device_id_type=MESH)

    def send_sums(h):
        lax.fori_loop(1, n, lambda d, _: (sum_copy(h, d).start(), 0)[1], 0)

    def out_copies(h):
        lanes = pl.ds(h * LANES, LANES)
        return (
            pltpu.make_async_copy(O1.at[h], pot_ref.at[0, :, :, lanes], out_sem.at[h, 0]),
            pltpu.make_async_copy(O2.at[h], res_ref.at[0, :, :, lanes], out_sem.at[h, 1]),
        )

    def finish(h):
        def arrive(d, _):
            place = S.at[h, (me + n - d) % n]
            pltpu.make_async_remote_copy(
                src_ref=place, dst_ref=place, send_sem=sum_send.at[h, d],
                recv_sem=sum_recv.at[h, d], device_id={"tile": (me + d) % n},
                device_id_type=MESH).wait_recv()
            return 0

        lax.fori_loop(1, n, arrive, 0)
        total = S[h, 0]
        for k in range(1, n):
            total = total + S[h, k]
        m0, m1, m2, m3, ex, er, ew = (total[k:k + 1] for k in range(7))
        a0 = m0 / m1
        next_norm = a0 * (a0 * m2 - m1)
        ratio = next_norm / m0
        curve = m1 - a0 * (2.0 * m2 - a0 * m3)
        a1 = next_norm / (curve - ratio * next_norm / a0)
        p = a0 + a1 * (1.0 + ratio)
        q = a1 * a0
        drop_ref[h:h + 1, :] = ex + p * er - q * ew
        p3, q3 = p[None], q[None]

        def last(t, _):
            c = pl.multiple_of(t * TILE, TILE)
            at = pl.ds(c + PAD, TILE)
            r = R[h, 2:2 + rows, at, :]
            w = W[h, 1:1 + rows, at, :]
            O1[h, :, pl.ds(c, TILE), :] = X[h, rows:2 * rows, at, :] + p3 * r - q3 * w
            O2[h, :, pl.ds(c, TILE), :] = r - p3 * w + q3 * U[h, :, pl.ds(c, TILE), :]
            return 0

        lax.fori_loop(0, cols // TILE, last, 0)
        for copy in out_copies(h):
            copy.start()

    for i in range(rows):
        take(0, i)
    relay_wait(0)
    for h in range(halves):
        compute(h)
        send_sums(h)
        if h + 1 < halves:
            for i in range(rows - 2):
                take(h + 1, i)
        finish(h)
        if h + 1 < halves:
            for i in range(rows - 2, rows):
                take(h + 1, i)
            relay_wait(h + 1)

    cond_each(lambda copy: copy.wait_send())
    for h in range(halves):
        side_copy(h).wait_send()
        for i in range(rows):
            row_copy(h, i).wait_send()

        @pl.when(can_relay)
        def _():
            for i in range(rows - 1):
                relay_copy(h, i).wait_send()

        lax.fori_loop(1, n, lambda d, _: (sum_copy(h, d).wait_send(), 0)[1], 0)
        for copy in out_copies(h):
            copy.wait()


def solution(mesh):
    n = mesh.shape["tile"]

    def shards(habitat, table, source_cell, ground_cell, start_potential):
        _, rows, cols, rhs = start_potential.shape
        halves = rhs // LANES
        width = cols + 2 * PAD
        f32 = jnp.float32
        dma = pltpu.SemaphoreType.DMA
        field = jax.ShapeDtypeStruct(start_potential.shape, f32)
        vmem = pl.BlockSpec(memory_space=pltpu.VMEM)
        hbm = pl.BlockSpec(memory_space=pltpu.HBM)
        potentials, residual, drop = pl.pallas_call(
            functools.partial(kernel, n, rows, cols),
            out_shape=(field, field, jax.ShapeDtypeStruct((halves, LANES), f32)),
            in_specs=[pl.BlockSpec(memory_space=pltpu.SMEM), vmem, vmem, vmem, hbm],
            out_specs=(hbm, hbm, vmem),
            scratch_shapes=[
                pltpu.VMEM((halves, 3 * rows, width, LANES), f32),
                pltpu.VMEM((halves, 2 * rows, width, LANES), f32),
                pltpu.VMEM((halves, 2 * rows - 2, width, LANES), f32),
                pltpu.VMEM((halves, rows, cols, LANES), f32),
                pltpu.VMEM((2 * rows + 1, width, LANES), f32),
                pltpu.VMEM((2 * rows, width, LANES), f32),
                pltpu.VMEM((2 * rows, width, LANES), f32),
                pltpu.VMEM((6, 2 * rows, cols), f32),
                pltpu.VMEM((width, LANES), f32),
                pltpu.VMEM((width, LANES), f32),
                pltpu.VMEM((width, LANES), f32),
                pltpu.VMEM((halves, n, TILE, LANES), f32),
                pltpu.VMEM((halves, rows, cols, LANES), f32),
                pltpu.VMEM((halves, rows, cols, LANES), f32),
                dma((halves,)),
                dma((5,)), dma((5,)),
                dma((halves,)), dma((halves,)),
                dma((halves, rows)), dma((halves, rows)),
                dma((halves, rows - 1)), dma((halves, rows - 1)),
                dma((halves, n)), dma((halves, n)),
                dma((halves, 2)),
            ],
            compiler_params=pltpu.CompilerParams(
                collective_id=0, has_side_effects=True, vmem_limit_bytes=48 * 2**20),
        )(table, habitat, source_cell.reshape(halves, LANES),
          ground_cell.reshape(halves, LANES), start_potential)
        return potentials, residual, drop.reshape(rhs)

    placed = (
        P(("grp", "tile"), None, None),
        P(),
        P("grp"),
        P("grp"),
        P(("grp", "tile"), None, None, None),
    )
    return jax.shard_map(
        shards,
        mesh=mesh,
        in_specs=placed,
        out_specs=(placed[4], placed[4], P("grp")),
        check_vma=False,
    )
```

time: 215 us -> 88.2 us (0.41)
  blocking collectives: 94 us -> 0 us
  Pallas kernels: 0 us -> 81.4 us
  waiting for transfers between devices: 44.4 us -> 0 us
  other arithmetic: 32.2 us -> 0 us
  starting transfers between devices: 24.4 us -> 0 us
  local copies, waits for them, and re-layouts: 19 us -> 5.9 us
    psum x3 -> x0, blocking collectives: 94 us -> none  [the longest x2 64.5 us: paired(): lax.psum((column_sums(field, field), column_sums(field, applied)), 'tile')]
    pallas_call x0 -> x1, Pallas kernels: none -> 81.4 us  [shards(): pl.pallas_call(functools.partial(kernel, n, rows, cols), out_shape=(field...]
    ppermute x12 -> x0, waiting for transfers between devices: 44.4 us -> none  [the longest x8 43.4 us: shifted(): return lax.ppermute(block, axis, route)]
    ppermute x12 -> x0, starting transfers between devices: 24.4 us -> none  [the longest x8 23.7 us: shifted(): return lax.ppermute(block, axis, route)]
    sub x4 -> x0, other arithmetic: 20.5 us -> none  [the longest x2 15.3 us: shards(): residual = residual - step_size * along]
    reduce_sum x4 -> x0, other arithmetic: 9.41 us -> none  [the longest x3 8.45 us: column_sums(): return jnp.sum(first * second, axis=(0, 1))]
    concatenate x7 -> x0, local copies, waits for them, and re-layouts: 8.67 us -> none  [the longest x5 6.32 us: operate(): leftward = jnp.concatenate([side[:, None], field[:, :-1]], 1)]
    slice x9 -> x0, local copies, waits for them, and re-layouts: 7.83 us -> none  [the longest x1 2.9 us: operate(): upper = jnp.concatenate([above[None], field[:-1]], 0)]
  transfers between devices with their start and end apart: 12 -> 0, of which waited for: 6 -> 0; matrix products, arithmetic and copies ran while one was open for 6% -> 0% of each run, Pallas kernels for 0% -> 0%
where the time goes in v1:
time: 88.2 us; the launch traced here: 88 us
  Pallas kernels  81.4 us (92%)
  local copies, waits for them, and re-layouts  5.9 us (7%)
    pallas_call x1, Pallas kernels, shards(): pl.pallas_call(functools.partial(kernel, n, rows, cols), out_shape=(field...  81.4 us
    unnamed x11, local copies, waits for them, and re-layouts  5.9 us

profile of v1, /device:TPU:0, one launch (start us, length us, event | category | flops | bytes accessed | tf_op | source)
XLA Modules:
  0.0 88.0 jit_solution(12209430982167696316)
XLA Ops:
  0.6 0.0 copy-start
  0.6 0.7 copy-done
  1.3 0.0 copy-start.1
  1.3 0.7 copy-done.1
  2.0 0.0 copy-start.2
  2.0 0.7 copy-done.2
  2.7 0.0 copy-start.3
  2.7 0.7 copy-done.3
  3.3 81.4 %shard_map.76 = (f32[1,4,512,256]{3,2,1,0:T(8,128)S(1)}, f32[1,4,512,256]{3,2,1,0:T(8,128)S(1)}, f32[2,128]{1,0:T(2,128)S(1)}) custom-call(f32[16]{0:T(128)S(1)} %copy-done.3, s32[1,4,512]{2,1,0:T(4,128)S(1)} %copy-done, s32[2,128]{1,0:T(2,128)S(1)} %bitcast.3, s32[2,128]{1,0:T(2,128)S(1)} %bitcast.4, f32[1,4,512,256]{3,2,1,0:T(8,128)} %start_ref.1), custom_call_target="tpu_custom_call" | custom-call | tf_op jit(solution)/shard_map/pallas_call | solution.py:394
  84.8 1.3 %copy.11 = f32[1,4,512,256]{3,2,1,0:T(8,128)} copy(f32[1,4,512,256]{3,2,1,0:T(8,128)S(1)} %get-tuple-element.12) | data formatting | bytes 4194304
  86.1 1.3 %copy.12 = f32[1,4,512,256]{3,2,1,0:T(8,128)} copy(f32[1,4,512,256]{3,2,1,0:T(8,128)S(1)} %get-tuple-element.13) | data formatting | bytes 4194304
  87.4 0.6 copy.13
Async XLA Ops:
  0.6 0.7 copy-start
  1.3 0.7 copy-start.1
  2.0 0.7 copy-start.2
  2.7 0.7 copy-start.3

commit v2 on v1

--- a/solution.py
+++ b/solution.py
@@ -15,9 +15,9 @@
 
 def kernel(n, rows, cols, table_ref, habitat_ref, source_ref, ground_ref, start_ref,
            pot_ref, res_ref, drop_ref,
-           X, R, W, U, V, H, D, C, T, TV, TH, S, O1, O2,
+           X, R, W, U, V, H, D, C, T, TV, TH, S,
            load_sem, cond_send, cond_recv, side_send, side_recv,
-           row_send, row_recv, relay_send, relay_recv, sum_send, sum_recv, out_sem):
+           row_send, row_recv, relay_send, relay_recv, sum_send, sum_recv):
     halves = X.shape[0]
     width = cols + 2 * PAD
     me = lax.axis_index("tile")
@@ -28,6 +28,9 @@
     side = me + 1 - 2 * core
     partner = me + 2 - 4 * odd
     own = pl.ds(PAD, cols)
+    travel = cols // TILE + 1
+    bounds = [0, travel * 19 // 65, travel * 37 // 65, travel * 53 // 65, travel]
+    pieces = len(bounds) - 1
 
     def load(h):
         return pltpu.make_async_copy(
@@ -110,59 +113,65 @@
             send_sem=side_send.at[h], recv_sem=side_recv.at[h],
             device_id={"tile": side}, device_id_type=MESH)
 
-    span = pl.ds(pl.multiple_of(PAD - core * TILE, TILE), cols + TILE)
-
-    def row_copy(h, i):
+    def span(j):
+        start = pl.multiple_of(PAD - core * TILE + bounds[j] * TILE, TILE)
+        return pl.ds(start, (bounds[j + 1] - bounds[j]) * TILE)
+
+    def row_copy(h, j, i):
         r = (i + odd) % rows
         return pltpu.make_async_remote_copy(
-            src_ref=X.at[h, rows + r, span, :], dst_ref=X.at[h, odd * 2 * rows + r, span, :],
-            send_sem=row_send.at[h, i], recv_sem=row_recv.at[h, i],
+            src_ref=X.at[h, rows + r, span(j), :],
+            dst_ref=X.at[h, odd * 2 * rows + r, span(j), :],
+            send_sem=row_send.at[h, j, i], recv_sem=row_recv.at[h, j, i],
             device_id={"tile": partner}, device_id_type=MESH)
 
-    def row_wait(h, i):
+    def row_wait(h, j, i):
         r = (i + 1 - odd) % rows
-        place = X.at[h, (1 - odd) * 2 * rows + r, span, :]
+        place = X.at[h, (1 - odd) * 2 * rows + r, span(j), :]
         pltpu.make_async_remote_copy(
-            src_ref=place, dst_ref=place, send_sem=row_send.at[h, i], recv_sem=row_recv.at[h, i],
+            src_ref=place, dst_ref=place,
+            send_sem=row_send.at[h, j, i], recv_sem=row_recv.at[h, j, i],
             device_id={"tile": partner}, device_id_type=MESH).wait_recv()
 
     relay_to = me + 4 - 8 * odd
     can_relay = jnp.where(odd == 0, chip + 2 < chips, chip >= 2)
     gets_relay = jnp.where(odd == 0, chip >= 2, chip + 2 < chips)
 
-    def relay_copy(h, i):
+    def relay_copy(h, j, i):
         src = (1 - odd) * (2 * rows + 1) + i
         dst = odd * 2 * rows + (1 - odd) + i
         return pltpu.make_async_remote_copy(
-            src_ref=X.at[h, src, span, :], dst_ref=X.at[h, dst, span, :],
-            send_sem=relay_send.at[h, i], recv_sem=relay_recv.at[h, i],
+            src_ref=X.at[h, src, span(j), :], dst_ref=X.at[h, dst, span(j), :],
+            send_sem=relay_send.at[h, j, i], recv_sem=relay_recv.at[h, j, i],
             device_id={"tile": relay_to}, device_id_type=MESH)
 
-    def relay_wait(h):
+    def relay_wait(h, j):
         @pl.when(gets_relay)
         def _():
             for i in range(rows - 1):
                 dst = odd * 2 * rows + (1 - odd) + i
-                place = X.at[h, dst, span, :]
+                place = X.at[h, dst, span(j), :]
                 pltpu.make_async_remote_copy(
-                    src_ref=place, dst_ref=place, send_sem=relay_send.at[h, i],
-                    recv_sem=relay_recv.at[h, i],
+                    src_ref=place, dst_ref=place, send_sem=relay_send.at[h, j, i],
+                    recv_sem=relay_recv.at[h, j, i],
                     device_id={"tile": relay_to}, device_id_type=MESH).wait_recv()
 
-    def take(h, i):
-        row_wait(h, i)
-        if i < rows - 1:
-            @pl.when(can_relay)
-            def _():
-                relay_copy(h, i).start()
+    def take(h, j):
+        for i in range(rows):
+            row_wait(h, j, i)
+            if i < rows - 1:
+                @pl.when(can_relay)
+                def _():
+                    relay_copy(h, j, i).start()
 
     for h in range(halves):
         load(h).wait()
         side_copy(h).start()
     for h in range(halves):
         side_copy(h).wait_recv()
-        for i in range(rows):
-            row_copy(h, i).start()
+        for j in range(pieces):
+            for i in range(rows):
+                row_copy(h, j, i).start()
 
     cond_copy(side, 2).wait_recv()
 
@@ -236,62 +245,80 @@
 
     lax.fori_loop(1, width // TILE - 1, spread, 0)
 
-    def cell_ids(c, count, top):
-        shape = (count, TILE, LANES)
-        r = chip * rows + top + lax.broadcasted_iota(jnp.int32, shape, 0)
-        col = core * cols - PAD + c + lax.broadcasted_iota(jnp.int32, shape, 1)
-        return r * total_cols + col
-
-    def applied(ref, h, skip, count, c, low, grounded):
+    tiles = width // TILE
+
+    def ends(lag, first, end):
+        return [first] + [PAD // TILE - core + bound - lag for bound in bounds[1:-1]] + [end]
+
+    r_ends = ends(1, 1, tiles - 1)
+    w_ends = ends(2, 1, tiles - 1)
+    u_ends = ends(3, 2, tiles - 2)
+
+    def shape_of(cells, h, top):
+        base = (chip * rows + top) * total_cols + core * cols - PAD
+        return jnp.broadcast_to(cells[h:h + 1, :] - base, (TILE, LANES))
+
+    def applied(ref, h, skip, count, c, low, grounds):
         at = pl.ds(c, TILE)
-        f = ref[h, skip:skip + count + 2, at, :]
-        left = ref[h, skip + 1:skip + 1 + count, pl.ds(c - 1, TILE), :]
-        right = ref[h, skip + 1:skip + 1 + count, pl.ds(c + 1, TILE), :]
-        mid = f[1:count + 1]
-        v = V[low:low + count + 1, at, :]
-        out = D[low:low + count, at, :] * mid + jnp.where(grounded, mid, 0.0)
-        out = out - v[:count] * f[:count] - v[1:] * f[2:]
-        out = out - H[low:low + count, pl.ds(c - 1, TILE), :] * left
-        return out - H[low:low + count, at, :] * right, mid
-
-    def compute(h):
-        src = source_ref[h:h + 1, :][None]
-        gnd = ground_ref[h:h + 1, :][None]
-        inner_rows = 2 * rows
+        west = pl.ds(c - 1, TILE)
+        east = pl.ds(c + 1, TILE)
+        column = c + lax.broadcasted_iota(jnp.int32, (TILE, LANES), 0)
+        mid = ref[h, skip + 1, at, :]
+        flow = V[low, at, :] * ref[h, skip, at, :]
+        for k in range(count):
+            after = ref[h, skip + k + 2, at, :]
+            v = V[low + k + 1, at, :]
+            grounded = column == grounds[k]
+            diag = D[low + k, at, :]
+            out = jnp.where(grounded, diag + 1.0, diag) * mid - flow
+            out = out - v * after
+            out = out - H[low + k, west, :] * ref[h, skip + 1 + k, west, :]
+            out = out - H[low + k, at, :] * ref[h, skip + 1 + k, east, :]
+            yield k, out, mid, grounded, column
+            flow = v * mid
+            mid = after
+
+    def zeros():
+        return tuple(jnp.zeros((TILE, LANES), jnp.float32) for _ in range(7))
+
+    def compute(h, j, acc):
+        def named(cells, top, count):
+            return [shape_of(cells, h, top + k) for k in range(count)]
+
+        count_r, count_w = 2 * rows, 2 * rows - 2
+        src_r, gnd_r = named(source_ref, -2, count_r), named(ground_ref, -2, count_r)
+        gnd_w = named(ground_ref, -1, count_w)
+        src_u, gnd_u = named(source_ref, 0, rows), named(ground_ref, 0, rows)
 
         def pass_r(t, _):
             c = pl.multiple_of(t * TILE, TILE)
-            ids = cell_ids(c, inner_rows, -2)
-            a, _mid = applied(X, h, 1, inner_rows, c, 0, ids == gnd)
-            R[h, :, pl.ds(c, TILE), :] = jnp.where(ids == src, 1.0, 0.0) - a
+            for k, a, _mid, _g, column in applied(X, h, 1, count_r, c, 0, gnd_r):
+                R[h, k, pl.ds(c, TILE), :] = jnp.where(column == src_r[k], 1.0 - a, -a)
             return 0
 
         def pass_w(t, _):
             c = pl.multiple_of(t * TILE, TILE)
-            count = inner_rows - 2
-            ids = cell_ids(c, count, -1)
-            a, _mid = applied(R, h, 0, count, c, 1, ids == gnd)
-            W[h, :, pl.ds(c, TILE), :] = a
+            for k, a, _mid, _g, _column in applied(R, h, 0, count_w, c, 1, gnd_w):
+                W[h, k, pl.ds(c, TILE), :] = a
             return 0
 
         def pass_u(t, acc):
             c = pl.multiple_of(t * TILE, TILE)
             at = pl.ds(c, TILE)
-            ids = cell_ids(c, rows, 0)
-            is_g = ids == gnd
-            u, w = applied(W, h, 0, rows, c, 2, is_g)
-            U[h, :, pl.ds(c - PAD, TILE), :] = u
-            r = R[h, 2:2 + rows, at, :]
-            x = X[h, rows:2 * rows, at, :]
-            sign = jnp.where(ids == src, 1.0, 0.0) - jnp.where(is_g, 1.0, 0.0)
-            terms = (r * r, r * w, w * w, w * u, sign * x, sign * r, sign * w)
-            return tuple(s + jnp.sum(term, axis=0) for s, term in zip(acc, terms))
-
-        tiles = width // TILE
-        lax.fori_loop(1, tiles - 1, pass_r, 0)
-        lax.fori_loop(1, tiles - 1, pass_w, 0)
-        acc = lax.fori_loop(2, tiles - 2, pass_u,
-                            tuple(jnp.zeros((TILE, LANES), jnp.float32) for _ in range(7)))
+            for k, u, w, grounded, column in applied(W, h, 0, rows, c, 2, gnd_u):
+                U[h, k, pl.ds(c - PAD, TILE), :] = u
+                r = R[h, 2 + k, at, :]
+                x = X[h, rows + k, at, :]
+                sign = jnp.where(column == src_u[k], 1.0, 0.0) - jnp.where(grounded, 1.0, 0.0)
+                terms = (r * r, r * w, w * w, w * u, sign * x, sign * r, sign * w)
+                acc = tuple(s + term for s, term in zip(acc, terms))
+            return acc
+
+        lax.fori_loop(r_ends[j], r_ends[j + 1], pass_r, 0)
+        lax.fori_loop(w_ends[j], w_ends[j + 1], pass_w, 0)
+        return lax.fori_loop(u_ends[j], u_ends[j + 1], pass_u, acc)
+
+    def keep(h, acc):
         sums = [jnp.sum(s, axis=0, keepdims=True) for s in acc]
         S[h, me] = jnp.concatenate(sums + [jnp.zeros((1, LANES), jnp.float32)], 0)
 
@@ -303,13 +330,6 @@
 
     def send_sums(h):
         lax.fori_loop(1, n, lambda d, _: (sum_copy(h, d).start(), 0)[1], 0)
-
-    def out_copies(h):
-        lanes = pl.ds(h * LANES, LANES)
-        return (
-            pltpu.make_async_copy(O1.at[h], pot_ref.at[0, :, :, lanes], out_sem.at[h, 0]),
-            pltpu.make_async_copy(O2.at[h], res_ref.at[0, :, :, lanes], out_sem.at[h, 1]),
-        )
 
     def finish(h):
         def arrive(d, _):
@@ -335,48 +355,54 @@
         drop_ref[h:h + 1, :] = ex + p * er - q * ew
         p3, q3 = p[None], q[None]
 
+        lanes = slice(h * LANES, (h + 1) * LANES)
+        p1 = jnp.broadcast_to(p, (TILE, LANES))
+        q1 = jnp.broadcast_to(q, (TILE, LANES))
+
         def last(t, _):
             c = pl.multiple_of(t * TILE, TILE)
             at = pl.ds(c + PAD, TILE)
-            r = R[h, 2:2 + rows, at, :]
-            w = W[h, 1:1 + rows, at, :]
-            O1[h, :, pl.ds(c, TILE), :] = X[h, rows:2 * rows, at, :] + p3 * r - q3 * w
-            O2[h, :, pl.ds(c, TILE), :] = r - p3 * w + q3 * U[h, :, pl.ds(c, TILE), :]
+            to = pl.ds(c, TILE)
+            for k in range(rows):
+                r = R[h, 2 + k, at, :]
+                w = W[h, 1 + k, at, :]
+                pot_ref[0, k, to, lanes] = X[h, rows + k, at, :] + p1 * r - q1 * w
+                res_ref[0, k, to, lanes] = r - p1 * w + q1 * U[h, k, to, :]
             return 0
 
         lax.fori_loop(0, cols // TILE, last, 0)
-        for copy in out_copies(h):
-            copy.start()
-
-    for i in range(rows):
-        take(0, i)
-    relay_wait(0)
-    for h in range(halves):
-        compute(h)
-        send_sums(h)
-        if h + 1 < halves:
-            for i in range(rows - 2):
-                take(h + 1, i)
-        finish(h)
-        if h + 1 < halves:
-            for i in range(rows - 2, rows):
-                take(h + 1, i)
-            relay_wait(h + 1)
+
+    order = [(h, j) for h in range(halves) for j in range(pieces)]
+    acc = zeros()
+    take(*order[0])
+    for now, following in zip(order, order[1:] + [None]):
+        h, j = now
+        if following is not None:
+            take(*following)
+        relay_wait(h, j)
+        acc = compute(h, j, acc)
+        if j == pieces - 1:
+            keep(h, acc)
+            send_sums(h)
+            acc = zeros()
+        if h > 0 and j == 1:
+            finish(h - 1)
+    finish(halves - 1)
 
     cond_each(lambda copy: copy.wait_send())
     for h in range(halves):
         side_copy(h).wait_send()
-        for i in range(rows):
-            row_copy(h, i).wait_send()
+        for j in range(pieces):
+            for i in range(rows):
+                row_copy(h, j, i).wait_send()
 
         @pl.when(can_relay)
         def _():
-            for i in range(rows - 1):
-                relay_copy(h, i).wait_send()
+            for j in range(pieces):
+                for i in range(rows - 1):
+                    relay_copy(h, j, i).wait_send()
 
         lax.fori_loop(1, n, lambda d, _: (sum_copy(h, d).wait_send(), 0)[1], 0)
-        for copy in out_copies(h):
-            copy.wait()
 
 
 def solution(mesh):
@@ -395,7 +421,7 @@
             functools.partial(kernel, n, rows, cols),
             out_shape=(field, field, jax.ShapeDtypeStruct((halves, LANES), f32)),
             in_specs=[pl.BlockSpec(memory_space=pltpu.SMEM), vmem, vmem, vmem, hbm],
-            out_specs=(hbm, hbm, vmem),
+            out_specs=(vmem, vmem, vmem),
             scratch_shapes=[
                 pltpu.VMEM((halves, 3 * rows, width, LANES), f32),
                 pltpu.VMEM((halves, 2 * rows, width, LANES), f32),
@@ -409,15 +435,12 @@
                 pltpu.VMEM((width, LANES), f32),
                 pltpu.VMEM((width, LANES), f32),
                 pltpu.VMEM((halves, n, TILE, LANES), f32),
-                pltpu.VMEM((halves, rows, cols, LANES), f32),
-                pltpu.VMEM((halves, rows, cols, LANES), f32),
                 dma((halves,)),
                 dma((5,)), dma((5,)),
                 dma((halves,)), dma((halves,)),
-                dma((halves, rows)), dma((halves, rows)),
-                dma((halves, rows - 1)), dma((halves, rows - 1)),
+                dma((halves, 4, rows)), dma((halves, 4, rows)),
+                dma((halves, 4, rows - 1)), dma((halves, 4, rows - 1)),
                 dma((halves, n)), dma((halves, n)),
-                dma((halves, 2)),
             ],
             compiler_params=pltpu.CompilerParams(
                 collective_id=0, has_side_effects=True, vmem_limit_bytes=48 * 2**20),

time: 88.2 us -> 76.9 us (0.87)
  Pallas kernels: 81.4 us -> 70.1 us
    pallas_call x1, Pallas kernels: 81.4 us -> 70.1 us  [shards(): pl.pallas_call(functools.partial(kernel, n, rows, cols), out_shape=(field...]
where the time goes in v2:
time: 76.9 us; the launch traced here: 76.6 us
  Pallas kernels  70.1 us (91%)
  local copies, waits for them, and re-layouts  5.9 us (8%)
    pallas_call x1, Pallas kernels, shards(): pl.pallas_call(functools.partial(kernel, n, rows, cols), out_shape=(field...  70.1 us
    unnamed x11, local copies, waits for them, and re-layouts  5.9 us

profile of v2, /device:TPU:0, one launch (start us, length us, event | category | flops | bytes accessed | tf_op | source)
XLA Modules:
  0.0 76.6 jit_solution(17550266180979063592)
XLA Ops:
  0.6 0.0 copy-start
  0.6 0.7 copy-done
  1.3 0.0 copy-start.1
  1.3 0.7 copy-done.1
  2.0 0.0 copy-start.2
  2.0 0.7 copy-done.2
  2.7 0.0 copy-start.3
  2.7 0.7 copy-done.3
  3.3 70.1 %shard_map.76 = (f32[1,4,512,256]{3,2,1,0:T(8,128)S(1)}, f32[1,4,512,256]{3,2,1,0:T(8,128)S(1)}, f32[2,128]{1,0:T(2,128)S(1)}) custom-call(f32[16]{0:T(128)S(1)} %copy-done.3, s32[1,4,512]{2,1,0:T(4,128)S(1)} %copy-done, s32[2,128]{1,0:T(2,128)S(1)} %bitcast.3, s32[2,128]{1,0:T(2,128)S(1)} %bitcast.4, f32[1,4,512,256]{3,2,1,0:T(8,128)} %start_ref.1), custom_call_target="tpu_custom_call" | custom-call | tf_op jit(solution)/shard_map/pallas_call | solution.py:420
  73.4 1.3 %copy.11 = f32[1,4,512,256]{3,2,1,0:T(8,128)} copy(f32[1,4,512,256]{3,2,1,0:T(8,128)S(1)} %get-tuple-element.12) | data formatting | bytes 4194304
  74.7 1.3 %copy.12 = f32[1,4,512,256]{3,2,1,0:T(8,128)} copy(f32[1,4,512,256]{3,2,1,0:T(8,128)S(1)} %get-tuple-element.13) | data formatting | bytes 4194304
  76.1 0.6 copy.13
Async XLA Ops:
  0.6 0.7 copy-start
  1.3 0.7 copy-start.1
  2.0 0.7 copy-start.2
  2.7 0.7 copy-start.3

commit v3 on v2

--- a/solution.py
+++ b/solution.py
@@ -13,10 +13,10 @@
 MESH = pl.DeviceIdType.MESH
 
 
-def kernel(n, rows, cols, table_ref, habitat_ref, source_ref, ground_ref, start_ref,
+def kernel(n, rows, cols, table_hbm, habitat_hbm, source_hbm, ground_hbm, start_ref,
            pot_ref, res_ref, drop_ref,
            X, R, W, U, V, H, D, C, T, TV, TH, S,
-           load_sem, cond_send, cond_recv, side_send, side_recv,
+           table_ref, habitat_ref, source_ref, ground_ref, small_sem, load_sem, cond_send, cond_recv, side_send, side_recv,
            row_send, row_recv, relay_send, relay_recv, sum_send, sum_recv):
     halves = X.shape[0]
     width = cols + 2 * PAD
@@ -37,6 +37,14 @@
             start_ref.at[0, :, :, pl.ds(h * LANES, LANES)], X.at[h, pl.ds(rows, rows), own, :],
             load_sem.at[h])
 
+    smalls = [
+        pltpu.make_async_copy(src, dst, small_sem.at[k])
+        for k, (src, dst) in enumerate((
+            (table_hbm, table_ref), (habitat_hbm, habitat_ref),
+            (source_hbm, source_ref), (ground_hbm, ground_ref)))
+    ]
+    for copy in smalls:
+        copy.start()
     for h in range(halves):
         load(h).start()
 
@@ -46,14 +54,8 @@
         pl.semaphore_signal(barrier, inc=1, device_id={"tile": (me + d) % n}, device_id_type=MESH)
         return 0
 
-    cells = habitat_ref[0]
-    cond = jnp.zeros(cells.shape, jnp.float32)
-    for level in range(table_ref.shape[0]):
-        cond = jnp.where(cells == level, table_ref[level], cond)
     for slot in range(5):
         C[slot] = jnp.zeros(C.shape[1:], jnp.float32)
-    C[5, 0:rows, :] = cond
-    C[5, rows:2 * rows, :] = cond
 
     def zero(ref, lead, c):
         count = ref.shape[1]
@@ -78,6 +80,16 @@
             X[h, 2 * rows:3 * rows] = jnp.zeros((rows, width, LANES), jnp.float32)
 
     lax.fori_loop(1, n, greet, 0)
+
+    for copy in smalls:
+        copy.wait()
+    cells = habitat_ref[0]
+    cond = jnp.zeros(cells.shape, jnp.float32)
+    for level in range(table_ref.shape[0]):
+        cond = jnp.where(cells == level, table_ref[level], cond)
+    C[5, 0:rows, :] = cond
+    C[5, rows:2 * rows, :] = cond
+
     pl.semaphore_wait(barrier, n - 1)
 
     def cond_copy(target, slot):
@@ -156,20 +168,26 @@
                     recv_sem=relay_recv.at[h, j, i],
                     device_id={"tile": relay_to}, device_id_type=MESH).wait_recv()
 
-    def take(h, j):
-        for i in range(rows):
+    order = [(h, j) for h in range(halves) for j in range(pieces)]
+    arrivals = [(h, j, i) for h, j in order for i in range(rows)]
+
+    def take(count):
+        for h, j, i in arrivals[:count]:
             row_wait(h, j, i)
             if i < rows - 1:
                 @pl.when(can_relay)
                 def _():
                     relay_copy(h, j, i).start()
+        del arrivals[:count]
 
     for h in range(halves):
         load(h).wait()
         side_copy(h).start()
-    for h in range(halves):
-        side_copy(h).wait_recv()
         for j in range(pieces):
+            if j in (0, pieces - 1):
+                @pl.when(core == (1 if j == 0 else 0))
+                def _():
+                    side_copy(h).wait_recv()
             for i in range(rows):
                 row_copy(h, j, i).start()
 
@@ -226,7 +244,8 @@
 
     TH[0:TILE, :] = jnp.zeros((TILE, LANES), jnp.float32)
     H[:, 0:TILE, :] = jnp.zeros((H.shape[0], TILE, LANES), jnp.float32)
-    lax.fori_loop(1, width // TILE - 1, edges, 0)
+    lax.fori_loop(1, width // TILE - 1, edges, 0, unroll=2)
+    take(2)
 
     def spread(t, _):
         c = pl.multiple_of(t * TILE, TILE)
@@ -243,7 +262,12 @@
             D[k, at, :] = jnp.broadcast_to(diag[:, k + 2:k + 3], shape)
         return 0
 
-    lax.fori_loop(1, width // TILE - 1, spread, 0)
+    parts = 6
+    for part in range(parts):
+        step = (width // TILE - 2) // parts
+        stop = width // TILE - 1 if part == parts - 1 else 1 + (part + 1) * step
+        lax.fori_loop(1 + part * step, stop, spread, 0)
+        take(1)
 
     tiles = width // TILE
 
@@ -372,13 +396,9 @@
 
         lax.fori_loop(0, cols // TILE, last, 0)
 
-    order = [(h, j) for h in range(halves) for j in range(pieces)]
     acc = zeros()
-    take(*order[0])
-    for now, following in zip(order, order[1:] + [None]):
-        h, j = now
-        if following is not None:
-            take(*following)
+    for k, (h, j) in enumerate(order):
+        take(max(0, len(arrivals) - rows * max(0, len(order) - k - 2)))
         relay_wait(h, j)
         acc = compute(h, j, acc)
         if j == pieces - 1:
@@ -420,7 +440,7 @@
         potentials, residual, drop = pl.pallas_call(
             functools.partial(kernel, n, rows, cols),
             out_shape=(field, field, jax.ShapeDtypeStruct((halves, LANES), f32)),
-            in_specs=[pl.BlockSpec(memory_space=pltpu.SMEM), vmem, vmem, vmem, hbm],
+            in_specs=[hbm] * 5,
             out_specs=(vmem, vmem, vmem),
             scratch_shapes=[
                 pltpu.VMEM((halves, 3 * rows, width, LANES), f32),
@@ -435,6 +455,11 @@
                 pltpu.VMEM((width, LANES), f32),
                 pltpu.VMEM((width, LANES), f32),
                 pltpu.VMEM((halves, n, TILE, LANES), f32),
+                pltpu.SMEM(table.shape, f32),
+                pltpu.VMEM(habitat.shape, jnp.int32),
+                pltpu.VMEM((halves, LANES), jnp.int32),
+                pltpu.VMEM((halves, LANES), jnp.int32),
+                dma((4,)),
                 dma((halves,)),
                 dma((5,)), dma((5,)),
                 dma((halves,)), dma((halves,)),
@@ -444,8 +469,9 @@
             ],
             compiler_params=pltpu.CompilerParams(
                 collective_id=0, has_side_effects=True, vmem_limit_bytes=48 * 2**20),
-        )(table, habitat, source_cell.reshape(halves, LANES),
-          ground_cell.reshape(halves, LANES), start_potential)
+        )(*(pltpu.with_memory_space_constraint(value, pltpu.HBM) for value in (
+            table, habitat, source_cell.reshape(halves, LANES),
+            ground_cell.reshape(halves, LANES), start_potential)))
         return potentials, residual, drop.reshape(rhs)
 
     placed = (

time: 76.9 us -> 73.1 us (0.951)
  local copies, waits for them, and re-layouts: 5.9 us -> 3.2 us
  Pallas kernels: 70.1 us -> 69.1 us
    unnamed x11 -> x3, local copies, waits for them, and re-layouts: 5.9 us -> 3.2 us
    pallas_call x1, Pallas kernels: 70.1 us -> 69.1 us  [shards(): pl.pallas_call(functools.partial(kernel, n, rows, cols), out_shape=(field...]
where the time goes in v3:
time: 73.1 us; the launch traced here: 72.9 us
  Pallas kernels  69.1 us (95%)
  local copies, waits for them, and re-layouts  3.2 us (4%)
    pallas_call x1, Pallas kernels, shards(): pl.pallas_call(functools.partial(kernel, n, rows, cols), out_shape=(field...  69.1 us
    unnamed x3, local copies, waits for them, and re-layouts  3.2 us

profile of v3, /device:TPU:0, one launch (start us, length us, event | category | flops | bytes accessed | tf_op | source)
XLA Modules:
  0.0 72.9 jit_solution(6127987211317766742)
XLA Ops:
  0.6 69.1 %shard_map.76 = (f32[1,4,512,256]{3,2,1,0:T(8,128)S(1)}, f32[1,4,512,256]{3,2,1,0:T(8,128)S(1)}, f32[2,128]{1,0:T(2,128)S(1)}) custom-call(f32[16]{0:T(128)} %table_hbm.1, s32[1,4,512]{2,1,0:T(4,128)} %habitat_hbm.1, s32[2,128]{1,0:T(2,128)} %bitcast.4, s32[2,128]{1,0:T(2,128)} %bitcast.5, f32[1,4,512,256]{3,2,1,0:T(8,128)} %start_ref.1), custom_call_target="tpu_custom_call" | custom-call | tf_op jit(solution)/shard_map/pallas_call | solution.py:440
  69.7 1.3 %copy.11 = f32[1,4,512,256]{3,2,1,0:T(8,128)} copy(f32[1,4,512,256]{3,2,1,0:T(8,128)S(1)} %get-tuple-element.12) | data formatting | bytes 4194304
  71.0 1.3 %copy.12 = f32[1,4,512,256]{3,2,1,0:T(8,128)} copy(f32[1,4,512,256]{3,2,1,0:T(8,128)S(1)} %get-tuple-element.13) | data formatting | bytes 4194304
  72.4 0.6 copy.13

commit v4 on v3

--- a/solution.py
+++ b/solution.py
@@ -61,24 +61,6 @@
         count = ref.shape[1]
         ref[lead[0], :, c:c + TILE, :] = jnp.zeros((count, TILE, LANES), jnp.float32)
 
-    for h in range(halves):
-        for c in (0, width - TILE):
-            zero(X, (h,), c)
-            zero(R, (h,), c)
-            zero(W, (h,), c)
-        @pl.when(core == 0)
-        def _():
-            zero(X, (h,), TILE)
-        @pl.when(core == 1)
-        def _():
-            zero(X, (h,), width - PAD)
-        @pl.when(chip == 0)
-        def _():
-            X[h, 0:rows] = jnp.zeros((rows, width, LANES), jnp.float32)
-        @pl.when(chip == chips - 1)
-        def _():
-            X[h, 2 * rows:3 * rows] = jnp.zeros((rows, width, LANES), jnp.float32)
-
     lax.fori_loop(1, n, greet, 0)
 
     for copy in smalls:
@@ -169,7 +151,9 @@
                     device_id={"tile": relay_to}, device_id_type=MESH).wait_recv()
 
     order = [(h, j) for h in range(halves) for j in range(pieces)]
-    arrivals = [(h, j, i) for h, j in order for i in range(rows)]
+    arrivals = [(h, j, i) for h, j in order[:-2] for i in range(rows)]
+    arrivals += [(h, j, i) for h, j in order[-2:] for i in range(rows - 1)]
+    arrivals += [(h, j, rows - 1) for h, j in order[-2:]]
 
     def take(count):
         for h, j, i in arrivals[:count]:
@@ -183,13 +167,30 @@
     for h in range(halves):
         load(h).wait()
         side_copy(h).start()
-        for j in range(pieces):
-            if j in (0, pieces - 1):
+        for j, i in [place[1:] for place in arrivals if place[0] == h]:
+            if i == 0 and j in (0, pieces - 1):
                 @pl.when(core == (1 if j == 0 else 0))
                 def _():
                     side_copy(h).wait_recv()
-            for i in range(rows):
-                row_copy(h, j, i).start()
+            row_copy(h, j, i).start()
+
+    for h in range(halves):
+        for c in (0, width - TILE):
+            zero(X, (h,), c)
+            zero(R, (h,), c)
+            zero(W, (h,), c)
+        @pl.when(core == 0)
+        def _():
+            zero(X, (h,), TILE)
+        @pl.when(core == 1)
+        def _():
+            zero(X, (h,), width - PAD)
+        @pl.when(chip == 0)
+        def _():
+            X[h, 0:rows] = jnp.zeros((rows, width, LANES), jnp.float32)
+        @pl.when(chip == chips - 1)
+        def _():
+            X[h, 2 * rows:3 * rows] = jnp.zeros((rows, width, LANES), jnp.float32)
 
     cond_copy(side, 2).wait_recv()
 
@@ -398,7 +399,8 @@
 
     acc = zeros()
     for k, (h, j) in enumerate(order):
-        take(max(0, len(arrivals) - rows * max(0, len(order) - k - 2)))
+        left = len(order) - k - 1
+        take(len(arrivals) - (left if left < 2 else rows * (left - 1)))
         relay_wait(h, j)
         acc = compute(h, j, acc)
         if j == pieces - 1:

time: 73.1 us -> 71.3 us (0.975)
  Pallas kernels: 69.1 us -> 67.3 us
    pallas_call x1, Pallas kernels: 69.1 us -> 67.3 us  [shards(): pl.pallas_call(functools.partial(kernel, n, rows, cols), out_shape=(field...]
where the time goes in v4:
time: 71.3 us; the launch traced here: 71.2 us
  Pallas kernels  67.3 us (94%)
  local copies, waits for them, and re-layouts  3.2 us (4%)
    pallas_call x1, Pallas kernels, shards(): pl.pallas_call(functools.partial(kernel, n, rows, cols), out_shape=(field...  67.3 us
    unnamed x3, local copies, waits for them, and re-layouts  3.2 us

profile of v4, /device:TPU:0, one launch (start us, length us, event | category | flops | bytes accessed | tf_op | source)
XLA Modules:
  0.0 71.2 jit_solution(4778920058115734710)
XLA Ops:
  0.6 67.3 %shard_map.76 = (f32[1,4,512,256]{3,2,1,0:T(8,128)S(1)}, f32[1,4,512,256]{3,2,1,0:T(8,128)S(1)}, f32[2,128]{1,0:T(2,128)S(1)}) custom-call(f32[16]{0:T(128)} %table_hbm.1, s32[1,4,512]{2,1,0:T(4,128)} %habitat_hbm.1, s32[2,128]{1,0:T(2,128)} %bitcast.4, s32[2,128]{1,0:T(2,128)} %bitcast.5, f32[1,4,512,256]{3,2,1,0:T(8,128)} %start_ref.1), custom_call_target="tpu_custom_call" | custom-call | tf_op jit(solution)/shard_map/pallas_call | solution.py:442
  68.0 1.3 %copy.11 = f32[1,4,512,256]{3,2,1,0:T(8,128)} copy(f32[1,4,512,256]{3,2,1,0:T(8,128)S(1)} %get-tuple-element.12) | data formatting | bytes 4194304
  69.3 1.3 %copy.12 = f32[1,4,512,256]{3,2,1,0:T(8,128)} copy(f32[1,4,512,256]{3,2,1,0:T(8,128)S(1)} %get-tuple-element.13) | data formatting | bytes 4194304
  70.6 0.6 copy.13
